TPU v7x, 256 devices: a whole 4x4x8 slice. The times are simulated.
256 devices in a mesh: ctx: 64 (over z, x, core), heads: 4 (over y).
Axes of the slice: x: 4, y: 4, z: 8, core: 2. Of those that a mesh axis runs over, the one named last changes fastest.
Arguments:
- query_rows: bfloat16 [64, 16, 2, 128], P('ctx', 'heads'), may hold values from -6 to 6
- past_keys: bfloat16 [64, 16, 4096, 128], P(None, 'heads', 'ctx'), may hold values from -6 to 6
- past_values: bfloat16 [64, 16, 4096, 128], P(None, 'heads', 'ctx'), may hold values from -6 to 6
- used_length: int32 [64], replicated, may hold values from 2048 to 4096
Outputs:
- read: bfloat16 [64, 16, 2, 128], P('ctx', 'heads')
All inputs are finite; a program needn't handle non-finite values.
Results may differ from a plain program's by a relative error of at most 0.0015.
Values may be sent and summed in bfloat16 or wider, within the bound.
A program may use at most 64 MiB of HBM per device.

v0:
```python
import jax
import jax.numpy as jnp
from jax import lax
from jax.sharding import Mesh
from jax.sharding import PartitionSpec as P

HEAD_SIZE = 128
CTX = ("ctx_0", "ctx_1", "ctx_2")


def gathered_by_axis(value, axes, dim):
    for axis in reversed(axes):
        value = lax.all_gather(value, axis, axis=dim, tiled=True)
    return value


def body(query_rows, past_keys, past_values, used_length):
    all_queries = gathered_by_axis(query_rows, CTX, 0)
    logit = jnp.einsum(
        "bkgd,bktd->bkgt", all_queries, past_keys, preferred_element_type=jnp.float32
    ) * HEAD_SIZE ** (-0.5)
    positions = lax.axis_index(CTX) * past_keys.shape[2] + jnp.arange(past_keys.shape[2])
    filled = positions[None, :] < used_length[:, None]
    logit = jnp.where(filled[:, None, None, :], logit, -1e30)
    top = jnp.max(logit, axis=-1)
    part = jnp.where(filled[:, None, None, :], jnp.exp(logit - top[..., None]), 0.0)
    weight_sum = jnp.sum(part, axis=-1)
    read_sum = jnp.einsum(
        "bkgt,bktd->bkgd", part, past_values.astype(jnp.float32), precision=lax.Precision.HIGHEST
    )
    tops, sums, parts = (
        lax.all_to_all(top[None], CTX, split_axis=1, concat_axis=0, tiled=True),
        lax.all_to_all(weight_sum[None], CTX, split_axis=1, concat_axis=0, tiled=True),
        lax.all_to_all(read_sum[None], CTX, split_axis=1, concat_axis=0, tiled=True),
    )
    best = jnp.max(tops, axis=0)
    scale = jnp.exp(tops - best)
    weight_own = jnp.sum(sums * scale, axis=0)
    read_own = jnp.sum(parts * scale[..., None], axis=0)
    read = (read_own / weight_own[..., None]).astype(jnp.bfloat16)
    return read


def solution(mesh):
    finer = Mesh(
        mesh.devices.reshape(8, 4, 2, mesh.shape["heads"]), ("ctx_0", "ctx_1", "ctx_2", "heads")
    )
    return jax.shard_map(
        body,
        mesh=finer,
        in_specs=(
            P(CTX, "heads", None, None),
            P(None, "heads", CTX, None),
            P(None, "heads", CTX, None),
            P(),
        ),
        out_specs=P(CTX, "heads", None, None),
        check_vma=False,
    )
```

profile of v0, /device:TPU:8, one launch (start us, length us, event | category | flops | bytes accessed | tf_op | source)
XLA Modules:
  0.0 102.9 jit_solution(3401453398949490919)
XLA Ops:
  0.0 0.7 copy.10
  0.7 1.8 %all_gather.9 = bf16[2,4,2,128]{3,1,2,0:T(4,128)(2,1)S(1)} all-gather(bf16[1,4,2,128]{3,1,2,0:T(4,128)(2,1)S(1)} %copy.10), channel_id=1, replica_groups=mesh['ctx_0'=8,'ctx_1'=4,'ctx_2'=2,'heads'=4] {'ctx_2'}, dimensions={0}, use_global_device_ids=true | all-gather | bytes 6144 | tf_op jit(solution)/shard_map/all_gather | solution.py:13
  2.5 12.2 %all_gather.10 = bf16[8,4,2,128]{3,1,2,0:T(4,128)(2,1)S(1)} all-gather(bf16[2,4,2,128]{3,1,2,0:T(4,128)(2,1)S(1)} %all_gather.9), channel_id=1, replica_groups=mesh['ctx_0'=8,'ctx_1'=4,'ctx_2'=2,'heads'=4] {'ctx_1'}, dimensions={0}, use_global_device_ids=true | all-gather | bytes 20480 | tf_op jit(solution)/shard_map/all_gather | solution.py:13
  14.7 28.2 %all_gather.11 = bf16[64,4,2,128]{3,1,2,0:T(4,128)(2,1)S(1)} all-gather(bf16[8,4,2,128]{3,1,2,0:T(4,128)(2,1)S(1)} %all_gather.10), channel_id=1, replica_groups=mesh['ctx_0'=8,'ctx_1'=4,'ctx_2'=2,'heads'=4] {'ctx_0'}, dimensions={0}, use_global_device_ids=true | all-gather | bytes 147456 | tf_op jit(solution)/shard_map/all_gather | solution.py:13
  42.9 0.7 broadcast_compare_fusion
  43.6 4.6 %fusion.10 = (f32[64,4,2]{2,1,0:T(4,128)S(1)}, f32[64,4,2,64]{3,2,1,0:T(2,128)S(1)}) fusion(bf16[64,4,64,128]{3,2,1,0:T(8,128)(2,1)} %param.5, bf16[64,4,2,128]{3,1,2,0:T(4,128)(2,1)S(1)} %all_gather.11, pred[64,64]{1,0:T(8,128)(4,1)S(1)} %broadcast_compare_fusion), kind=kOutput, calls=%fused_computation.19 | convolution fusion | flops 8486400 | bytes 4462592 | tf_op jit(solution)/shard_map/bkgd,bktd->bkgt/dot_general | solution.py:19
  48.2 0.8 fusion.7
  49.0 1.1 %copy.15 = f32[1,64,4,2]{2,3,0,1:T(2,128)} copy(f32[1,64,4,2]{3,2,1,0:T(4,128)S(1)} %bitcast.33) | data formatting | bytes 4096 | tf_op jit(solution)/shard_map/broadcast_in_dim | solution.py:33
  50.1 7.7 %all-to-all-start.2 = ((f32[1,64,4,2]{2,3,0,1:T(2,128)}), f32[1,64,4,2]{2,3,0,1:T(2,128)S(1)}, u32[]{:S(2)}, u32[]{:S(2)}) async-start(f32[1,64,4,2]{2,3,0,1:T(2,128)} %copy.15), calls=%async_computation.2 | async-start | bytes 131072 | tf_op jit(solution)/shard_map/all_to_all | solution.py:33
  57.8 1.1 %copy.13 = f32[1,64,4,2]{2,3,0,1:T(2,128)} copy(f32[1,64,4,2]{3,2,1,0:T(4,128)S(1)} %bitcast.32) | data formatting | bytes 4096 | tf_op jit(solution)/shard_map/broadcast_in_dim | solution.py:32
  58.9 9.0 %all-to-all-done.2 = f32[1,64,4,2]{2,3,0,1:T(2,128)S(1)} async-done(((f32[1,64,4,2]{2,3,0,1:T(2,128)}), f32[1,64,4,2]{2,3,0,1:T(2,128)S(1)}, u32[]{:S(2)}, u32[]{:S(2)}) %all-to-all-start.2) | async-done | bytes 2080 | tf_op jit(solution)/shard_map/all_to_all | solution.py:33
  67.9 4.6 %all-to-all-start.1 = ((f32[1,64,4,2]{2,3,0,1:T(2,128)}), f32[1,64,4,2]{2,3,0,1:T(2,128)S(1)}, u32[]{:S(2)}, u32[]{:S(2)}) async-start(f32[1,64,4,2]{2,3,0,1:T(2,128)} %copy.13), calls=%async_computation.1 | async-start | bytes 131072 | tf_op jit(solution)/shard_map/all_to_all | solution.py:32
  72.6 5.9 %convolution_bitcast_fusion = f32[1,64,4,2,128]{4,3,2,0,1:T(2,128)} fusion(bf16[64,4,64,128]{3,2,1,0:T(8,128)(2,1)} %param.6, f32[64,4,2,64]{3,2,1,0:T(2,128)S(1)} %get-tuple-element.6, pred[64,64]{1,0:T(8,128)(4,1)S(1)} %broadcast_compare_fusion, f32[64,4,2]{2,1,0:T(4,128)S(1)} %get-tuple-element.5), kind=kOutput, calls=%fused_computation | convolution fusion | flops 50397184 | bytes 4593664 | tf_op jit(solution)/shard_map/bkgt,bktd->bkgd/dot_general | solution.py:28
  78.5 4.2 %all-to-all-done.1 = f32[1,64,4,2]{2,3,0,1:T(2,128)S(1)} async-done(((f32[1,64,4,2]{2,3,0,1:T(2,128)}), f32[1,64,4,2]{2,3,0,1:T(2,128)S(1)}, u32[]{:S(2)}, u32[]{:S(2)}) %all-to-all-start.1) | async-done | bytes 2080 | tf_op jit(solution)/shard_map/all_to_all | solution.py:32
  82.7 6.1 %all-to-all-start = ((f32[1,64,4,2,128]{4,3,2,0,1:T(2,128)}), f32[1,64,4,2,128]{4,3,2,0,1:T(2,128)S(1)}, u32[]{:S(2)}, u32[]{:S(2)}) async-start(f32[1,64,4,2,128]{4,3,2,0,1:T(2,128)} %convolution_bitcast_fusion), calls=%async_computation | async-start | bytes 524288 | tf_op jit(solution)/shard_map/all_to_all | solution.py:34
  88.8 0.1 reduce_max.19
  88.8 0.1 fusion.6
  88.9 0.1 copy.16
  89.1 0.5 copy.14
  89.6 12.4 %all-to-all-done = f32[1,64,4,2,128]{4,3,2,0,1:T(2,128)S(1)} async-done(((f32[1,64,4,2,128]{4,3,2,0,1:T(2,128)}), f32[1,64,4,2,128]{4,3,2,0,1:T(2,128)S(1)}, u32[]{:S(2)}, u32[]{:S(2)}) %all-to-all-start) | async-done | bytes 262176 | tf_op jit(solution)/shard_map/all_to_all | solution.py:34
  101.9 0.3 fusion.1
  102.3 0.7 fusion.8
  (2 shorter events, 0.0 us)
Async XLA Ops:
  50.1 17.8 %all-to-all-start.2 = ((f32[1,64,4,2]{2,3,0,1:T(2,128)}), f32[1,64,4,2]{2,3,0,1:T(2,128)S(1)}, u32[]{:S(2)}, u32[]{:S(2)}) async-start(f32[1,64,4,2]{2,3,0,1:T(2,128)} %copy.15), calls=%async_computation.2 | async-start | bytes 131072 | tf_op jit(solution)/shard_map/all_to_all | solution.py:33
  67.9 14.7 %all-to-all-start.1 = ((f32[1,64,4,2]{2,3,0,1:T(2,128)}), f32[1,64,4,2]{2,3,0,1:T(2,128)S(1)}, u32[]{:S(2)}, u32[]{:S(2)}) async-start(f32[1,64,4,2]{2,3,0,1:T(2,128)} %copy.13), calls=%async_computation.1 | async-start | bytes 131072 | tf_op jit(solution)/shard_map/all_to_all | solution.py:32
  82.7 19.3 %all-to-all-start = ((f32[1,64,4,2,128]{4,3,2,0,1:T(2,128)}), f32[1,64,4,2,128]{4,3,2,0,1:T(2,128)S(1)}, u32[]{:S(2)}, u32[]{:S(2)}) async-start(f32[1,64,4,2,128]{4,3,2,0,1:T(2,128)} %convolution_bitcast_fusion), calls=%async_computation | async-start | bytes 524288 | tf_op jit(solution)/shard_map/all_to_all | solution.py:34
where the time goes:
time: 104 us; the launch traced here: 103 us
  blocking collectives  42.2 us (41%)
  waiting for transfers between devices  25.6 us (25%)
  starting transfers between devices  18.4 us (18%)
  matrix products  10.5 us (10%)
  local copies, waits for them, and re-layouts  3.48 us (3%)
  other arithmetic  2.74 us (3%)
    all_gather x3, blocking collectives, gathered_by_axis(): value = lax.all_gather(value, axis, axis=dim, tiled=True)  42.2 us
    all_to_all x1, waiting for transfers between devices, body(): lax.all_to_all(read_sum[None], CTX, split_axis=1, concat_axis=0, tiled=True)  12.4 us
    all_to_all x1, waiting for transfers between devices, body(): lax.all_to_all(weight_sum[None], CTX, split_axis=1, concat_axis=0, tiled=...  9.04 us
    all_to_all x1, starting transfers between devices, body(): lax.all_to_all(weight_sum[None], CTX, split_axis=1, concat_axis=0, tiled=...  7.69 us
    all_to_all x1, starting transfers between devices, body(): lax.all_to_all(read_sum[None], CTX, split_axis=1, concat_axis=0, tiled=True)  6.09 us
    dot_general x1, matrix products, body(): jnp.einsum('bkgt,bktd->bkgd', part, past_values.astype(jnp.float32), prec...  5.91 us
    all_to_all x1, starting transfers between devices, body(): lax.all_to_all(top[None], CTX, split_axis=1, concat_axis=0, tiled=True)  4.6 us
    dot_general x1, matrix products, body(): jnp.einsum('bkgd,bktd->bkgt', all_queries, past_keys, preferred_element_t...  4.58 us
  transfers between devices with their start and end apart: 3, of which 3 were waited for; matrix products, arithmetic and copies ran while one was open for 8% of the time, Pallas kernels for 0%

commit v1 on v0

v1 whole, which is shorter than its diff:
```python
import jax
import jax.numpy as jnp
from jax import lax
from jax.experimental import pallas as pl
from jax.experimental.pallas import tpu as pltpu
from jax.sharding import PartitionSpec as P

MESH = pl.DeviceIdType.MESH
ZS, XS, CS = 8, 4, 2
STRETCHES = ZS * XS * CS
HEADS, GROUP, STRETCH, SIZE = 4, 2, 64, 128
ROWS, COLS = HEADS * GROUP, HEADS * STRETCH
MASKED = -1e30
BESIDE = [(x, c) for x in (0, 1, 3, 2) for c in range(CS)]


def ring_place(i):
    return lax.rem(jnp.where(lax.rem(i, 2) == 1, (i + 1) // 2, ZS - i // 2), ZS)


def ring_order(i):
    return jnp.where(i == 0, 0, jnp.where(i == ZS - 1, ZS - 1, jnp.where(lax.rem(i, 2) == 1, i + 1, i - 1)))


def kernel(query, keys, values, lengths, out, k_buf, v_buf, q_buf, len_buf, part, parts, q_send, q_recv, p_send, p_recv, k_sem, v_sem, in_sem):
    me = lax.axis_index("ctx")
    my_z, my_x, my_c = me // (XS * CS), lax.rem(me // CS, XS), lax.rem(me, CS)

    def owner(i, x, c):
        z = lax.rem(my_z + ring_place(i), ZS)
        return (z * XS + lax.rem(my_x + x, XS)) * CS + lax.rem(my_c + c, CS)

    def others(do):
        for x, c in BESIDE[1:]:
            do(0, x, c)

        @pl.loop(1, ZS)
        def _(i):
            for x, c in BESIDE:
                do(i, x, c)

    barrier = pltpu.get_barrier_semaphore()

    def greet(i, x, c):
        pl.semaphore_signal(barrier, inc=1, device_id={"ctx": owner(i, x, c)}, device_id_type=MESH)

    others(greet)
    own_copy = pltpu.make_async_copy(query, q_buf.at[me], in_sem.at[0])
    own_copy.start()
    len_copy = pltpu.make_async_copy(lengths, len_buf, in_sem.at[1])
    len_copy.start()
    k_copy = pltpu.make_async_copy(keys, k_buf, k_sem)
    k_copy.start()
    v_copy = pltpu.make_async_copy(values, v_buf, v_sem)
    v_copy.start()
    own_copy.wait()
    len_copy.wait()
    pl.semaphore_wait(barrier, STRETCHES - 1)

    def ask(i, x, c):
        pltpu.make_async_remote_copy(
            src_ref=q_buf.at[me],
            dst_ref=q_buf.at[me],
            send_sem=q_send,
            recv_sem=q_recv.at[ring_order(i)],
            device_id={"ctx": owner(i, x, c)},
            device_id_type=MESH,
        ).start()

    others(ask)
    k_copy.wait()
    v_copy.wait()

    row = lax.broadcasted_iota(jnp.int32, (ROWS, COLS), 0)
    col = lax.broadcasted_iota(jnp.int32, (ROWS, COLS), 1)
    own_head = row // GROUP == col // STRETCH
    position = me * STRETCH + lax.rem(col, STRETCH)
    slot_row = lax.broadcasted_iota(jnp.int32, (ROWS, SIZE), 0)
    slot = lax.broadcasted_iota(jnp.int32, (ROWS, SIZE), 1)

    def partial(b):
        logit = lax.dot_general(
            q_buf[b], k_buf[b], (((1,), (1,)), ((), ())), preferred_element_type=jnp.float32
        ) * SIZE ** (-0.5)
        filled = own_head & (position < len_buf[b])
        logit = jnp.where(filled, logit, MASKED)
        top = jnp.max(logit, axis=1, keepdims=True)
        share = jnp.where(filled, jnp.exp(logit - top), 0.0)
        weight = jnp.sum(share, axis=1, keepdims=True)
        coarse = share.astype(jnp.bfloat16).astype(jnp.float32)
        halves = jnp.concatenate([coarse, share - coarse], axis=0).astype(jnp.bfloat16)
        read = jnp.dot(halves, v_buf[b], preferred_element_type=jnp.float32)
        stats = jnp.where(slot == slot_row, top, jnp.where(slot == slot_row + ROWS, weight, 0.0))
        return read[:ROWS] + read[ROWS:], jnp.sum(stats, axis=0, keepdims=True)

    def answer(i, x, c):
        b = owner(i, x, c)
        read, stats = partial(b)
        part[b, pl.ds(0, ROWS), :] = read
        part[b, pl.ds(ROWS, 1), :] = stats

    def give(i, x, c):
        b = owner(i, x, c)
        pltpu.make_async_remote_copy(
            src_ref=part.at[b],
            dst_ref=parts.at[me],
            send_sem=p_send,
            recv_sem=p_recv,
            device_id={"ctx": b},
            device_id_type=MESH,
        ).start()

    def arrived(n, i):
        pltpu.make_async_copy(q_buf.at[pl.ds(0, n)], q_buf.at[pl.ds(0, n)], q_recv.at[i]).wait()

    read, stats = partial(me)
    parts[me, pl.ds(0, ROWS), :] = read
    parts[me, pl.ds(ROWS, 1), :] = stats
    arrived(len(BESIDE) - 1, 0)
    for x, c in BESIDE[1:]:
        answer(0, x, c)
    for x, c in BESIDE[1:]:
        give(0, x, c)

    @pl.loop(1, ZS)
    def _(i):
        arrived(len(BESIDE), i)
        for x, c in BESIDE:
            answer(i, x, c)
        for x, c in BESIDE:
            give(i, x, c)

    rest = pl.ds(0, STRETCHES - 1)
    pltpu.make_async_copy(parts.at[rest], parts.at[rest], p_recv).wait()

    stats = parts[:, ROWS, :]
    scale = jnp.exp(stats - jnp.max(stats, axis=0, keepdims=True))
    weight = jnp.sum(scale * pltpu.roll(stats, SIZE - ROWS, 1), axis=0, keepdims=True)
    scale = jnp.transpose(scale / weight)[:ROWS, :]
    total = jnp.zeros((ROWS, SIZE), jnp.float32)
    for s in range(STRETCHES):
        total += scale[:, s : s + 1] * parts[s, pl.ds(0, ROWS), :]
    out[...] = total.astype(out.dtype)

    pltpu.make_async_copy(q_buf.at[rest], q_buf.at[rest], q_send).wait()
    pltpu.make_async_copy(part.at[rest], part.at[rest], p_send).wait()


def body(query_rows, past_keys, past_values, used_length):
    anywhere = pl.BlockSpec(memory_space=pl.ANY)
    read = pl.pallas_call(
        kernel,
        out_shape=jax.ShapeDtypeStruct((ROWS, SIZE), jnp.bfloat16),
        in_specs=[anywhere] * 4,
        out_specs=pl.BlockSpec(memory_space=pltpu.VMEM),
        scratch_shapes=[
            pltpu.VMEM((STRETCHES, COLS, SIZE), jnp.bfloat16),
            pltpu.VMEM((STRETCHES, COLS, SIZE), jnp.bfloat16),
            pltpu.VMEM((STRETCHES, ROWS, SIZE), jnp.bfloat16),
            pltpu.SMEM((STRETCHES,), jnp.int32),
            pltpu.VMEM((STRETCHES, ROWS + 1, SIZE), jnp.float32),
            pltpu.VMEM((STRETCHES, ROWS + 1, SIZE), jnp.float32),
            pltpu.SemaphoreType.DMA,
            pltpu.SemaphoreType.DMA((ZS,)),
            pltpu.SemaphoreType.DMA,
            pltpu.SemaphoreType.DMA,
            pltpu.SemaphoreType.DMA,
            pltpu.SemaphoreType.DMA,
            pltpu.SemaphoreType.DMA((2,)),
        ],
        compiler_params=pltpu.CompilerParams(collective_id=0, has_side_effects=True),
    )(
        query_rows.reshape(ROWS, SIZE),
        past_keys.reshape(STRETCHES, COLS, SIZE),
        past_values.reshape(STRETCHES, COLS, SIZE),
        used_length,
    )
    return read.reshape(query_rows.shape)


def solution(mesh):
    return jax.shard_map(
        body,
        mesh=mesh,
        in_specs=(
            P("ctx", "heads", None, None),
            P(None, "heads", "ctx", None),
            P(None, "heads", "ctx", None),
            P(),
        ),
        out_specs=P("ctx", "heads", None, None),
        check_vma=False,
    )
```

time: 104 us -> 38.7 us (0.37)
  the two profiles are of different devices: /device:TPU:8 before, /device:TPU:1 now
where the time goes in v1:
time: 38.7 us; the launch traced here: 38.6 us
  Pallas kernels  37.3 us (96%)
  local copies, waits for them, and re-layouts  1.26 us (3%)
    pallas_call x1, Pallas kernels, body(): pl.pallas_call(kernel, out_shape=jax.ShapeDtypeStruct((ROWS, SIZE), jnp.b...  37.3 us
    unnamed x1, local copies, waits for them, and re-layouts  1.26 us

profile of v1, /device:TPU:1, one launch (start us, length us, event | category | flops | bytes accessed | tf_op | source)
XLA Modules:
  0.0 38.6 jit_solution(11225786485516516494)
XLA Ops:
  0.0 37.3 %shard_map.46 = bf16[8,128]{1,0:T(8,128)(2,1)} custom-call(bf16[8,128]{1,0:T(8,128)(2,1)} %bitcast.7, bf16[64,256,128]{2,1,0:T(8,128)(2,1)} %bitcast.4, bf16[64,256,128]{2,1,0:T(8,128)(2,1)} %bitcast.5, s32[64]{0:T(128)} %lengths.1), custom_call_target="tpu_custom_call" | custom-call | tf_op jit(solution)/shard_map/pallas_call | solution.py:151
  37.3 1.3 %copy.6 = bf16[1,4,2,128]{3,2,1,0:T(2,128)(2,1)} copy(bf16[1,4,2,128]{3,2,1,0:T(2,128)(2,1)} %bitcast.6) | data formatting | bytes 4096

commit v2 on v1

--- a/solution.py
+++ b/solution.py
@@ -11,38 +11,28 @@
 HEADS, GROUP, STRETCH, SIZE = 4, 2, 64, 128
 ROWS, COLS = HEADS * GROUP, HEADS * STRETCH
 MASKED = -1e30
-BESIDE = [(x, c) for x in (0, 1, 3, 2) for c in range(CS)]
-
-
-def ring_place(i):
-    return lax.rem(jnp.where(lax.rem(i, 2) == 1, (i + 1) // 2, ZS - i // 2), ZS)
-
-
-def ring_order(i):
-    return jnp.where(i == 0, 0, jnp.where(i == ZS - 1, ZS - 1, jnp.where(lax.rem(i, 2) == 1, i + 1, i - 1)))
+FAR = (4, 5, 3, 6, 2, 7, 1, 0)
+BESIDE = [(x, c) for x in (2, 1, 3, 0) for c in (1, 0)]
 
 
 def kernel(query, keys, values, lengths, out, k_buf, v_buf, q_buf, len_buf, part, parts, q_send, q_recv, p_send, p_recv, k_sem, v_sem, in_sem):
     me = lax.axis_index("ctx")
     my_z, my_x, my_c = me // (XS * CS), lax.rem(me // CS, XS), lax.rem(me, CS)
 
-    def owner(i, x, c):
-        z = lax.rem(my_z + ring_place(i), ZS)
+    def owner(z, x, c):
         return (z * XS + lax.rem(my_x + x, XS)) * CS + lax.rem(my_c + c, CS)
 
     def others(do):
-        for x, c in BESIDE[1:]:
-            do(0, x, c)
-
-        @pl.loop(1, ZS)
-        def _(i):
+        for step in FAR:
+            z = lax.rem(my_z + step, ZS)
             for x, c in BESIDE:
-                do(i, x, c)
+                if (step, x, c) != (0, 0, 0):
+                    do(owner(z, x, c))
 
     barrier = pltpu.get_barrier_semaphore()
 
-    def greet(i, x, c):
-        pl.semaphore_signal(barrier, inc=1, device_id={"ctx": owner(i, x, c)}, device_id_type=MESH)
+    def greet(b):
+        pl.semaphore_signal(barrier, inc=1, device_id={"ctx": b}, device_id_type=MESH)
 
     others(greet)
     own_copy = pltpu.make_async_copy(query, q_buf.at[me], in_sem.at[0])
@@ -57,13 +47,13 @@
     len_copy.wait()
     pl.semaphore_wait(barrier, STRETCHES - 1)
 
-    def ask(i, x, c):
+    def ask(b):
         pltpu.make_async_remote_copy(
             src_ref=q_buf.at[me],
             dst_ref=q_buf.at[me],
             send_sem=q_send,
-            recv_sem=q_recv.at[ring_order(i)],
-            device_id={"ctx": owner(i, x, c)},
+            recv_sem=q_recv.at[my_z],
+            device_id={"ctx": b},
             device_id_type=MESH,
         ).start()
 
@@ -78,58 +68,55 @@
     slot_row = lax.broadcasted_iota(jnp.int32, (ROWS, SIZE), 0)
     slot = lax.broadcasted_iota(jnp.int32, (ROWS, SIZE), 1)
 
-    def partial(b):
-        logit = lax.dot_general(
-            q_buf[b], k_buf[b], (((1,), (1,)), ((), ())), preferred_element_type=jnp.float32
-        ) * SIZE ** (-0.5)
-        filled = own_head & (position < len_buf[b])
-        logit = jnp.where(filled, logit, MASKED)
-        top = jnp.max(logit, axis=1, keepdims=True)
-        share = jnp.where(filled, jnp.exp(logit - top), 0.0)
-        weight = jnp.sum(share, axis=1, keepdims=True)
-        coarse = share.astype(jnp.bfloat16).astype(jnp.float32)
-        halves = jnp.concatenate([coarse, share - coarse], axis=0).astype(jnp.bfloat16)
-        read = jnp.dot(halves, v_buf[b], preferred_element_type=jnp.float32)
-        stats = jnp.where(slot == slot_row, top, jnp.where(slot == slot_row + ROWS, weight, 0.0))
-        return read[:ROWS] + read[ROWS:], jnp.sum(stats, axis=0, keepdims=True)
+    def answer(owners):
+        logits = [
+            lax.dot_general(q_buf[b], k_buf[b], (((1,), (1,)), ((), ())), preferred_element_type=jnp.float32)
+            for b in owners
+        ]
+        halves, tops, weights = [], [], []
+        for b, logit in zip(owners, logits):
+            filled = own_head & (position < len_buf[b])
+            logit = jnp.where(filled, logit * SIZE ** (-0.5), MASKED)
+            top = jnp.max(logit, axis=1, keepdims=True)
+            share = jnp.where(filled, jnp.exp(logit - top), 0.0)
+            coarse = share.astype(jnp.bfloat16).astype(jnp.float32)
+            halves.append(jnp.concatenate([coarse, share - coarse], axis=0).astype(jnp.bfloat16))
+            tops.append(top)
+            weights.append(jnp.sum(share, axis=1, keepdims=True))
+        reads = [jnp.dot(half, v_buf[b], preferred_element_type=jnp.float32) for b, half in zip(owners, halves)]
+        for b, read, top, weight in zip(owners, reads, tops, weights):
+            stats = jnp.where(slot == slot_row, top, jnp.where(slot == slot_row + ROWS, weight, 0.0))
+            part[b, pl.ds(0, ROWS), :] = read[:ROWS] + read[ROWS:]
+            part[b, pl.ds(ROWS, 1), :] = jnp.sum(stats, axis=0, keepdims=True)
 
-    def answer(i, x, c):
-        b = owner(i, x, c)
-        read, stats = partial(b)
-        part[b, pl.ds(0, ROWS), :] = read
-        part[b, pl.ds(ROWS, 1), :] = stats
+    def give(b):
+        @pl.when(b != me)
+        def _():
+            pltpu.make_async_remote_copy(
+                src_ref=part.at[b],
+                dst_ref=parts.at[me],
+                send_sem=p_send,
+                recv_sem=p_recv,
+                device_id={"ctx": b},
+                device_id_type=MESH,
+            ).start()
 
-    def give(i, x, c):
-        b = owner(i, x, c)
-        pltpu.make_async_remote_copy(
-            src_ref=part.at[b],
-            dst_ref=parts.at[me],
-            send_sem=p_send,
-            recv_sem=p_recv,
-            device_id={"ctx": b},
-            device_id_type=MESH,
-        ).start()
+    def arrived(z):
+        def wait(n):
+            pltpu.make_async_copy(q_buf.at[pl.ds(0, n)], q_buf.at[pl.ds(0, n)], q_recv.at[z]).wait()
 
-    def arrived(n, i):
-        pltpu.make_async_copy(q_buf.at[pl.ds(0, n)], q_buf.at[pl.ds(0, n)], q_recv.at[i]).wait()
+        pl.when(z == my_z)(lambda: wait(len(BESIDE) - 1))
+        pl.when(z != my_z)(lambda: wait(len(BESIDE)))
 
-    read, stats = partial(me)
-    parts[me, pl.ds(0, ROWS), :] = read
-    parts[me, pl.ds(ROWS, 1), :] = stats
-    arrived(len(BESIDE) - 1, 0)
-    for x, c in BESIDE[1:]:
-        answer(0, x, c)
-    for x, c in BESIDE[1:]:
-        give(0, x, c)
+    @pl.loop(0, ZS)
+    def _(z):
+        arrived(z)
+        owners = [owner(z, x, c) for x, c in BESIDE]
+        answer(owners)
+        for b in owners:
+            give(b)
 
-    @pl.loop(1, ZS)
-    def _(i):
-        arrived(len(BESIDE), i)
-        for x, c in BESIDE:
-            answer(i, x, c)
-        for x, c in BESIDE:
-            give(i, x, c)
-
+    parts[me] = part[me]
     rest = pl.ds(0, STRETCHES - 1)
     pltpu.make_async_copy(parts.at[rest], parts.at[rest], p_recv).wait()
 

time: 38.7 us -> 28.6 us (0.74)
  the two profiles are of different devices: /device:TPU:1 before, /device:TPU:192 now
where the time goes in v2:
time: 28.6 us; the launch traced here: 28.5 us
  Pallas kernels  27.2 us (95%)
  local copies, waits for them, and re-layouts  1.26 us (4%)
    pallas_call x1, Pallas kernels, body(): pl.pallas_call(kernel, out_shape=jax.ShapeDtypeStruct((ROWS, SIZE), jnp.b...  27.2 us
    unnamed x1, local copies, waits for them, and re-layouts  1.26 us

profile of v2, /device:TPU:192, one launch (start us, length us, event | category | flops | bytes accessed | tf_op | source)
XLA Modules:
  0.0 28.5 jit_solution(2291604946266217358)
XLA Ops:
  0.0 27.2 %shard_map.46 = bf16[8,128]{1,0:T(8,128)(2,1)} custom-call(bf16[8,128]{1,0:T(8,128)(2,1)} %bitcast.7, bf16[64,256,128]{2,1,0:T(8,128)(2,1)} %bitcast.4, bf16[64,256,128]{2,1,0:T(8,128)(2,1)} %bitcast.5, s32[64]{0:T(128)} %lengths.1), custom_call_target="tpu_custom_call" | custom-call | tf_op jit(solution)/shard_map/pallas_call | solution.py:138
  27.2 1.3 %copy.6 = bf16[1,4,2,128]{3,2,1,0:T(2,128)(2,1)} copy(bf16[1,4,2,128]{3,2,1,0:T(2,128)(2,1)} %bitcast.6) | data formatting | bytes 4096

commit v3 on v2

v3 whole, which is shorter than its diff:
```python
import jax
import jax.numpy as jnp
from jax import lax
from jax.experimental import pallas as pl
from jax.experimental.pallas import tpu as pltpu
from jax.sharding import PartitionSpec as P

MESH = pl.DeviceIdType.MESH
ZS, XS, CS = 8, 4, 2
STRETCHES = ZS * XS * CS
HEADS, GROUP, STRETCH, SIZE = 4, 2, 64, 128
ROWS, COLS = HEADS * GROUP, HEADS * STRETCH
MASKED = -1e30
CHIPS = ZS * XS
FAR = (4, 5, 3, 6, 2, 7, 1, 0)
ACROSS = (2, 1, 3, 0)
EARLY = 2
NEAREST = [min(range(EARLY), key=lambda e: min((z - e) % ZS, (e - z) % ZS)) for z in range(ZS)]


def kernel(
    query, keys, values, lengths, out, k_buf, v_buf, q_buf, len_buf, part, parts,
    q_send, q_recv, p_send, p_recv, k_own, v_own, k_send, v_send, k_recv, v_recv, in_sem, there, all_there,
):
    me = lax.axis_index("ctx")
    my_z, my_x, my_c = me // (XS * CS), lax.rem(me // CS, XS), lax.rem(me, CS)
    chip, beside = me // CS, me + 1 - 2 * my_c
    first = my_z < EARLY

    def turn(k):
        return jnp.where(k < ZS // 2, k, ZS + ZS // 2 - 1 - k)

    def device(z, x):
        return (z * XS + x) * CS + my_c

    def in_plane(z, do):
        for across in ACROSS:
            x = lax.rem(my_x + across, XS)
            if across:
                do(device(z, x))
            else:
                pl.when(z != my_z)(lambda: do(device(z, x)))

    def beyond(do):
        for step in FAR:
            z = lax.rem(my_z + step, ZS)
            pl.when(z >= EARLY)(lambda: in_plane(z, do))

    def within(do):
        for z in range(EARLY):
            in_plane(z, do)

    barrier = pltpu.get_barrier_semaphore()

    def tell(sem, b):
        pl.semaphore_signal(sem, inc=1, device_id={"ctx": b}, device_id_type=MESH)

    def greet(b):
        tell(barrier, b)

    greet(beside)

    @pl.when(first)
    def _():
        beyond(greet)
        within(greet)

    own_copy = pltpu.make_async_copy(query, q_buf.at[chip], in_sem.at[0])
    own_copy.start()
    len_copy = pltpu.make_async_copy(lengths, len_buf, in_sem.at[1])
    len_copy.start()
    k_copy = pltpu.make_async_copy(keys.at[:, my_c], k_buf.at[:, my_c], k_own)
    k_copy.start()
    v_copy = pltpu.make_async_copy(values.at[:, my_c], v_buf.at[:, my_c], v_own)
    v_copy.start()
    pl.when(first)(lambda: pl.semaphore_wait(barrier, EARLY * XS))

    @pl.when(~first)
    def _():
        pl.semaphore_wait(barrier, EARLY * XS + 1)
        within(lambda b: tell(there, b))

    own_copy.wait()
    len_copy.wait()

    def ask(b):
        pltpu.make_async_remote_copy(
            src_ref=q_buf.at[chip],
            dst_ref=q_buf.at[chip],
            send_sem=q_send,
            recv_sem=q_recv.at[my_z],
            device_id={"ctx": b},
            device_id_type=MESH,
        ).start()

    within(ask)

    def swap(z, source, buffer, send_sem, recv_sem):
        rows = pl.ds(z * XS, XS)
        return pltpu.make_async_remote_copy(
            src_ref=source.at[rows, 1 - my_c],
            dst_ref=buffer.at[rows, my_c],
            send_sem=send_sem,
            recv_sem=recv_sem.at[z],
            device_id={"ctx": beside},
            device_id_type=MESH,
        )

    @pl.loop(0, ZS)
    def _(k):
        swap(turn(k), keys, k_buf, k_send, k_recv).start()
        swap(turn(k), values, v_buf, v_send, v_recv).start()

    def arrived(z):
        def wait(n):
            pltpu.make_async_copy(q_buf.at[pl.ds(0, n)], q_buf.at[pl.ds(0, n)], q_recv.at[z]).wait()

        pl.when(z == my_z)(lambda: wait(XS - 1))
        pl.when(z != my_z)(lambda: wait(XS))

    @pl.when(first)
    def _():
        pl.semaphore_wait(there, (ZS - EARLY) * XS)
        for z in range(EARLY, ZS):
            pl.when(my_z == NEAREST[z])(lambda z=z: tell(all_there, device(z, my_x)))

    pl.when(~first)(lambda: pl.semaphore_wait(all_there, 1))
    beyond(ask)
    k_copy.wait()
    v_copy.wait()

    row = lax.broadcasted_iota(jnp.int32, (ROWS, COLS), 0)
    col = lax.broadcasted_iota(jnp.int32, (ROWS, COLS), 1)
    own_head = row // GROUP == col // STRETCH
    position = [(chip * CS + c) * STRETCH + lax.rem(col, STRETCH) for c in range(CS)]
    slot_row = lax.broadcasted_iota(jnp.int32, (ROWS, SIZE), 0)
    slot = lax.broadcasted_iota(jnp.int32, (ROWS, SIZE), 1)

    def answer(z):
        owners = [z * XS + x for x in range(XS)]
        logits = [
            [
                lax.dot_general(q_buf[i], k_buf[i, c], (((1,), (1,)), ((), ())), preferred_element_type=jnp.float32)
                for c in range(CS)
            ]
            for i in owners
        ]
        halves, tops, weights = [], [], []
        for i, pair in zip(owners, logits):
            length = len_buf[i * CS + my_c]
            filled = [own_head & (position[c] < length) for c in range(CS)]
            pair = [jnp.where(f, logit * SIZE ** (-0.5), MASKED) for f, logit in zip(filled, pair)]
            top = jnp.max(jnp.maximum(*pair), axis=1, keepdims=True)
            shares = [jnp.where(f, jnp.exp(logit - top), 0.0) for f, logit in zip(filled, pair)]
            coarse = [share.astype(jnp.bfloat16).astype(jnp.float32) for share in shares]
            halves.append(
                [jnp.concatenate([c, share - c], axis=0).astype(jnp.bfloat16) for c, share in zip(coarse, shares)]
            )
            tops.append(top)
            weights.append(jnp.sum(shares[0] + shares[1], axis=1, keepdims=True))
        reads = [
            sum(jnp.dot(halves_of[c], v_buf[i, c], preferred_element_type=jnp.float32) for c in range(CS))
            for i, halves_of in zip(owners, halves)
        ]
        for i, read, top, weight in zip(owners, reads, tops, weights):
            stats = jnp.where(slot == slot_row, top, jnp.where(slot == slot_row + ROWS, weight, 0.0))
            part[i, pl.ds(0, ROWS), :] = read[:ROWS] + read[ROWS:]
            part[i, pl.ds(ROWS, 1), :] = jnp.sum(stats, axis=0, keepdims=True)

    def give(b):
        pltpu.make_async_remote_copy(
            src_ref=part.at[b // CS],
            dst_ref=parts.at[chip],
            send_sem=p_send,
            recv_sem=p_recv,
            device_id={"ctx": b},
            device_id_type=MESH,
        ).start()

    @pl.loop(0, ZS)
    def _(k):
        z = turn(k)
        arrived(z)
        swap(z, keys, k_buf, k_send, k_recv).wait_recv()
        swap(z, values, v_buf, v_send, v_recv).wait_recv()
        answer(z)
        in_plane(z, give)

    parts[chip] = part[chip]

    rest = pl.ds(0, CHIPS - 1)
    pltpu.make_async_copy(parts.at[rest], parts.at[rest], p_recv).wait()

    stats = parts[:, ROWS, :]
    scale = jnp.exp(stats - jnp.max(stats, axis=0, keepdims=True))
    weight = jnp.sum(scale * pltpu.roll(stats, SIZE - ROWS, 1), axis=0, keepdims=True)
    scale = jnp.transpose(scale / weight)[:ROWS, :]
    total = jnp.zeros((ROWS, SIZE), jnp.float32)
    for s in range(CHIPS):
        total += scale[:, s : s + 1] * parts[s, pl.ds(0, ROWS), :]
    out[...] = total.astype(out.dtype)

    pltpu.make_async_copy(q_buf.at[rest], q_buf.at[rest], q_send).wait()
    pltpu.make_async_copy(part.at[rest], part.at[rest], p_send).wait()
    pltpu.make_async_copy(k_buf.at[:, 0], k_buf.at[:, 0], k_send).wait()
    pltpu.make_async_copy(v_buf.at[:, 0], v_buf.at[:, 0], v_send).wait()


def body(query_rows, past_keys, past_values, used_length):
    anywhere = pl.BlockSpec(memory_space=pl.ANY)
    dma = pltpu.SemaphoreType.DMA
    read = pl.pallas_call(
        kernel,
        out_shape=jax.ShapeDtypeStruct((ROWS, SIZE), jnp.bfloat16),
        in_specs=[anywhere] * 4,
        out_specs=pl.BlockSpec(memory_space=pltpu.VMEM),
        scratch_shapes=[
            pltpu.VMEM((CHIPS, CS, COLS, SIZE), jnp.bfloat16),
            pltpu.VMEM((CHIPS, CS, COLS, SIZE), jnp.bfloat16),
            pltpu.VMEM((CHIPS, ROWS, SIZE), jnp.bfloat16),
            pltpu.SMEM((STRETCHES,), jnp.int32),
            pltpu.VMEM((CHIPS, ROWS + 1, SIZE), jnp.float32),
            pltpu.VMEM((CHIPS, ROWS + 1, SIZE), jnp.float32),
            dma, dma((ZS,)), dma, dma, dma, dma, dma, dma, dma((ZS,)), dma((ZS,)), dma((2,)),
            pltpu.SemaphoreType.REGULAR, pltpu.SemaphoreType.REGULAR,
        ],
        compiler_params=pltpu.CompilerParams(collective_id=0, has_side_effects=True),
    )(
        query_rows.reshape(ROWS, SIZE),
        past_keys.reshape(CHIPS, CS, COLS, SIZE),
        past_values.reshape(CHIPS, CS, COLS, SIZE),
        used_length,
    )
    return read.reshape(query_rows.shape)


def solution(mesh):
    return jax.shard_map(
        body,
        mesh=mesh,
        in_specs=(
            P("ctx", "heads", None, None),
            P(None, "heads", "ctx", None),
            P(None, "heads", "ctx", None),
            P(),
        ),
        out_specs=P("ctx", "heads", None, None),
        check_vma=False,
    )
```

time: 28.6 us -> 24.5 us (0.86)
  the two profiles are of different devices: /device:TPU:192 before, /device:TPU:8 now
where the time goes in v3:
time: 24.5 us; the launch traced here: 24.4 us
  Pallas kernels  23.1 us (94%)
  local copies, waits for them, and re-layouts  1.26 us (5%)
    pallas_call x1, Pallas kernels, body(): pl.pallas_call(kernel, out_shape=jax.ShapeDtypeStruct((ROWS, SIZE), jnp.b...  23.1 us
    unnamed x1, local copies, waits for them, and re-layouts  1.26 us

profile of v3, /device:TPU:8, one launch (start us, length us, event | category | flops | bytes accessed | tf_op | source)
XLA Modules:
  0.0 24.4 jit_solution(11653942892990107505)
XLA Ops:
  0.0 23.1 %shard_map.46 = bf16[8,128]{1,0:T(8,128)(2,1)} custom-call(bf16[8,128]{1,0:T(8,128)(2,1)} %bitcast.7, bf16[32,2,256,128]{3,2,1,0:T(8,128)(2,1)} %bitcast.4, bf16[32,2,256,128]{3,2,1,0:T(8,128)(2,1)} %bitcast.5, s32[64]{0:T(128)} %lengths.1), custom_call_target="tpu_custom_call" | custom-call | tf_op jit(solution)/shard_map/pallas_call | solution.py:212
  23.1 1.3 %copy.6 = bf16[1,4,2,128]{3,2,1,0:T(2,128)(2,1)} copy(bf16[1,4,2,128]{3,2,1,0:T(2,128)(2,1)} %bitcast.6) | data formatting | bytes 4096

commit v4 on v3

--- a/solution.py
+++ b/solution.py
@@ -211,7 +211,7 @@
     dma = pltpu.SemaphoreType.DMA
     read = pl.pallas_call(
         kernel,
-        out_shape=jax.ShapeDtypeStruct((ROWS, SIZE), jnp.bfloat16),
+        out_shape=pltpu.VMEM((ROWS, SIZE), jnp.bfloat16),
         in_specs=[anywhere] * 4,
         out_specs=pl.BlockSpec(memory_space=pltpu.VMEM),
         scratch_shapes=[

time: 24.5 us -> 23.2 us (0.947)
  local copies, waits for them, and re-layouts: 1.26 us -> 0.58 us
  Pallas kernels: 23.1 us -> 22.5 us
    unnamed x1, local copies, waits for them, and re-layouts: 1.26 us -> 0.58 us
    pallas_call x1, Pallas kernels: 23.1 us -> 22.5 us  [body(): pl.pallas_call(kernel, out_shape=pltpu.VMEM((ROWS, SIZE), jnp.bfloat16),...]
where the time goes in v4:
time: 23.2 us; the launch traced here: 23.1 us
  Pallas kernels  22.5 us (97%)
  local copies, waits for them, and re-layouts  0.58 us (2%)
    pallas_call x1, Pallas kernels, body(): pl.pallas_call(kernel, out_shape=pltpu.VMEM((ROWS, SIZE), jnp.bfloat16),...  22.5 us
    unnamed x1, local copies, waits for them, and re-layouts  0.58 us

profile of v4, /device:TPU:8, one launch (start us, length us, event | category | flops | bytes accessed | tf_op | source)
XLA Modules:
  0.0 23.1 jit_solution(1543473204232049135)
XLA Ops:
  0.0 22.5 %shard_map.46 = bf16[8,128]{1,0:T(8,128)(2,1)S(1)} custom-call(bf16[8,128]{1,0:T(8,128)(2,1)} %bitcast.7, bf16[32,2,256,128]{3,2,1,0:T(8,128)(2,1)} %bitcast.5, bf16[32,2,256,128]{3,2,1,0:T(8,128)(2,1)} %bitcast.6, s32[64]{0:T(128)} %lengths.1), custom_call_target="tpu_custom_call" | custom-call | tf_op jit(solution)/shard_map/pallas_call | solution.py:212
  22.5 0.6 %copy.6 = bf16[1,4,2,128]{3,2,1,0:T(2,128)(2,1)} copy(bf16[1,4,2,128]{3,2,1,0:T(2,128)(2,1)S(1)} %bitcast.4) | data formatting | bytes 4096

commit v5 on v4

--- a/solution.py
+++ b/solution.py
@@ -14,18 +14,17 @@
 CHIPS = ZS * XS
 FAR = (4, 5, 3, 6, 2, 7, 1, 0)
 ACROSS = (2, 1, 3, 0)
-EARLY = 2
-NEAREST = [min(range(EARLY), key=lambda e: min((z - e) % ZS, (e - z) % ZS)) for z in range(ZS)]
+SOON = ZS // 2
 
 
 def kernel(
     query, keys, values, lengths, out, k_buf, v_buf, q_buf, len_buf, part, parts,
-    q_send, q_recv, p_send, p_recv, k_own, v_own, k_send, v_send, k_recv, v_recv, in_sem, there, all_there,
+    q_send, q_recv, p_send, p_recv, k_own, v_own, k_send, v_send, k_recv, v_recv, in_sem, there, column, x_there, x_all,
 ):
     me = lax.axis_index("ctx")
     my_z, my_x, my_c = me // (XS * CS), lax.rem(me // CS, XS), lax.rem(me, CS)
     chip, beside = me // CS, me + 1 - 2 * my_c
-    first = my_z < EARLY
+    soon = my_z < SOON
 
     def turn(k):
         return jnp.where(k < ZS // 2, k, ZS + ZS // 2 - 1 - k)
@@ -41,14 +40,13 @@
             else:
                 pl.when(z != my_z)(lambda: do(device(z, x)))
 
-    def beyond(do):
-        for step in FAR:
-            z = lax.rem(my_z + step, ZS)
-            pl.when(z >= EARLY)(lambda: in_plane(z, do))
-
-    def within(do):
-        for z in range(EARLY):
-            in_plane(z, do)
+    def in_column(planes, do):
+        for z in planes:
+            pl.when(z != my_z)(lambda z=z: do(device(z, my_x)))
+
+    def beside_x(do):
+        for across in ACROSS[:-1]:
+            do(device(my_z, lax.rem(my_x + across, XS)))
 
     barrier = pltpu.get_barrier_semaphore()
 
@@ -60,10 +58,15 @@
 
     greet(beside)
 
-    @pl.when(first)
-    def _():
-        beyond(greet)
-        within(greet)
+    pl.when(soon | (my_x == 0))(lambda: beside_x(greet))
+
+    @pl.when(my_z == 0)
+    def _():
+        for z in range(SOON, ZS):
+            in_plane(z, greet)
+        in_column(range(1, SOON), greet)
+
+    pl.when(my_z == 1)(lambda: in_column(range(2, ZS), greet))
 
     own_copy = pltpu.make_async_copy(query, q_buf.at[chip], in_sem.at[0])
     own_copy.start()
@@ -73,12 +76,13 @@
     k_copy.start()
     v_copy = pltpu.make_async_copy(values.at[:, my_c], v_buf.at[:, my_c], v_own)
     v_copy.start()
-    pl.when(first)(lambda: pl.semaphore_wait(barrier, EARLY * XS))
-
-    @pl.when(~first)
-    def _():
-        pl.semaphore_wait(barrier, EARLY * XS + 1)
-        within(lambda b: tell(there, b))
+    pl.when(my_z == 0)(lambda: pl.semaphore_wait(barrier, XS))
+    pl.when(my_z == 1)(lambda: pl.semaphore_wait(barrier, XS + 1))
+    pl.when((my_z >= 2) & (soon | (my_x == 0)))(lambda: pl.semaphore_wait(barrier, XS + 2))
+    pl.when(~soon & (my_x != 0))(lambda: pl.semaphore_wait(barrier, XS + 3))
+    pl.when(my_z >= 1)(lambda: tell(there, device(0, my_x)))
+    pl.when(my_z >= 2)(lambda: tell(there, device(1, my_x)))
+    pl.when(~soon & (my_x != 0))(lambda: tell(x_there, device(my_z, 0)))
 
     own_copy.wait()
     len_copy.wait()
@@ -93,7 +97,8 @@
             device_id_type=MESH,
         ).start()
 
-    within(ask)
+    pl.when(soon)(lambda: beside_x(ask))
+    pl.when(~soon)(lambda: in_plane(0, ask))
 
     def swap(z, source, buffer, send_sem, recv_sem):
         rows = pl.ds(z * XS, XS)
@@ -118,14 +123,44 @@
         pl.when(z == my_z)(lambda: wait(XS - 1))
         pl.when(z != my_z)(lambda: wait(XS))
 
-    @pl.when(first)
-    def _():
-        pl.semaphore_wait(there, (ZS - EARLY) * XS)
-        for z in range(EARLY, ZS):
-            pl.when(my_z == NEAREST[z])(lambda z=z: tell(all_there, device(z, my_x)))
-
-    pl.when(~first)(lambda: pl.semaphore_wait(all_there, 1))
-    beyond(ask)
+    def bundle(b):
+        rows = pl.ds(my_z * XS, XS)
+        pltpu.make_async_remote_copy(
+            src_ref=q_buf.at[rows],
+            dst_ref=q_buf.at[rows],
+            send_sem=q_send,
+            recv_sem=q_recv.at[my_z],
+            device_id={"ctx": b},
+            device_id_type=MESH,
+        ).start()
+
+    @pl.when(~soon)
+    def _():
+        @pl.when(my_x == 0)
+        def _():
+            pl.semaphore_wait(x_there, XS - 1)
+            beside_x(lambda b: tell(x_all, b))
+
+        pl.when(my_x != 0)(lambda: pl.semaphore_wait(x_all, 1))
+        beside_x(ask)
+
+    arrived(my_z)
+
+    @pl.when(my_z == 0)
+    def _():
+        pl.semaphore_wait(there, ZS - 1)
+        in_column(range(SOON, ZS), lambda b: tell(column, b))
+
+    @pl.when(my_z == 1)
+    def _():
+        pl.semaphore_wait(there, ZS - 2)
+        in_column(range(2, SOON), lambda b: tell(column, b))
+
+    pl.when(my_z >= 2)(lambda: pl.semaphore_wait(column, 1))
+    for step in FAR[:-1]:
+        z = lax.rem(my_z + step, ZS)
+        pl.when(soon | (z != 0))(lambda z=z: bundle(device(z, my_x)))
+
     k_copy.wait()
     v_copy.wait()
 
@@ -180,7 +215,7 @@
     @pl.loop(0, ZS)
     def _(k):
         z = turn(k)
-        arrived(z)
+        pl.when(z != my_z)(lambda: arrived(z))
         swap(z, keys, k_buf, k_send, k_recv).wait_recv()
         swap(z, values, v_buf, v_send, v_recv).wait_recv()
         answer(z)
@@ -222,7 +257,7 @@
             pltpu.VMEM((CHIPS, ROWS + 1, SIZE), jnp.float32),
             pltpu.VMEM((CHIPS, ROWS + 1, SIZE), jnp.float32),
             dma, dma((ZS,)), dma, dma, dma, dma, dma, dma, dma((ZS,)), dma((ZS,)), dma((2,)),
-            pltpu.SemaphoreType.REGULAR, pltpu.SemaphoreType.REGULAR,
+            *[pltpu.SemaphoreType.REGULAR] * 4,
         ],
         compiler_params=pltpu.CompilerParams(collective_id=0, has_side_effects=True),
     )(

time: 23.2 us -> 21.2 us (0.914)
  Pallas kernels: 22.5 us -> 20.4 us
    pallas_call x1, Pallas kernels: 22.5 us -> 20.4 us  [body(): pl.pallas_call(kernel, out_shape=pltpu.VMEM((ROWS, SIZE), jnp.bfloat16),...]
where the time goes in v5:
time: 21.2 us; the launch traced here: 21 us
  Pallas kernels  20.4 us (96%)
  local copies, waits for them, and re-layouts  0.58 us (3%)
    pallas_call x1, Pallas kernels, body(): pl.pallas_call(kernel, out_shape=pltpu.VMEM((ROWS, SIZE), jnp.bfloat16),...  20.4 us
    unnamed x1, local copies, waits for them, and re-layouts  0.58 us

profile of v5, /device:TPU:8, one launch (start us, length us, event | category | flops | bytes accessed | tf_op | source)
XLA Modules:
  0.0 21.0 jit_solution(11921243789727552634)
XLA Ops:
  0.0 20.4 %shard_map.46 = bf16[8,128]{1,0:T(8,128)(2,1)S(1)} custom-call(bf16[8,128]{1,0:T(8,128)(2,1)} %bitcast.7, bf16[32,2,256,128]{3,2,1,0:T(8,128)(2,1)} %bitcast.5, bf16[32,2,256,128]{3,2,1,0:T(8,128)(2,1)} %bitcast.6, s32[64]{0:T(128)} %lengths.1), custom_call_target="tpu_custom_call" | custom-call | tf_op jit(solution)/shard_map/pallas_call | solution.py:247
  20.4 0.6 %copy.6 = bf16[1,4,2,128]{3,2,1,0:T(2,128)(2,1)} copy(bf16[1,4,2,128]{3,2,1,0:T(2,128)(2,1)S(1)} %bitcast.4) | data formatting | bytes 4096

commit v6 on v5

--- a/solution.py
+++ b/solution.py
@@ -16,21 +16,46 @@
 ACROSS = (2, 1, 3, 0)
 SOON = ZS // 2
 
+ORDERS = (
+    (0, 1, 2, 3, 4, 5, 6, 7),
+    (0, 1, 2, 3, 5, 4, 6, 7),
+    (0, 1, 2, 3, 6, 5, 7, 4),
+    (0, 1, 2, 3, 7, 6, 5, 4),
+    (0, 1, 2, 3, 4, 5, 6, 7),
+    (0, 1, 2, 3, 5, 6, 4, 7),
+    (0, 1, 2, 3, 6, 5, 7, 4),
+    (0, 1, 2, 3, 7, 6, 5, 4),
+)
 
 def kernel(
     query, keys, values, lengths, out, k_buf, v_buf, q_buf, len_buf, part, parts,
-    q_send, q_recv, p_send, p_recv, k_own, v_own, k_send, v_send, k_recv, v_recv, in_sem, there, column, x_there, x_all,
+    q_send, q_recv, p_send, p_recv, k_own, v_own, k_send, v_send, k_recv, v_recv, in_sem, there, column, x_there, x_all, late_recv,
 ):
     me = lax.axis_index("ctx")
     my_z, my_x, my_c = me // (XS * CS), lax.rem(me // CS, XS), lax.rem(me, CS)
     chip, beside = me // CS, me + 1 - 2 * my_c
     soon = my_z < SOON
 
-    def turn(k):
-        return jnp.where(k < ZS // 2, k, ZS + ZS // 2 - 1 - k)
+    def in_order(do):
+        order = 0
+        for z, planes in enumerate(ORDERS):
+            order = jnp.where(my_z == z, sum(p * ZS**k for k, p in enumerate(planes)), order)
+
+        def step(k, order):
+            do(k, lax.rem(order, ZS))
+            return order // ZS
+
+        lax.fori_loop(0, ZS, step, order)
 
     def device(z, x):
         return (z * XS + x) * CS + my_c
+
+    hub = (my_z * XS) * CS + 1
+
+    def spokes(do):
+        for x in range(1, XS):
+            for c in range(CS):
+                do((my_z * XS + x) * CS + c)
 
     def in_plane(z, do):
         for across in ACROSS:
@@ -58,7 +83,8 @@
 
     greet(beside)
 
-    pl.when(soon | (my_x == 0))(lambda: beside_x(greet))
+    pl.when(soon)(lambda: beside_x(greet))
+    pl.when(~soon & (me == hub))(lambda: spokes(greet))
 
     @pl.when(my_z == 0)
     def _():
@@ -82,7 +108,7 @@
     pl.when(~soon & (my_x != 0))(lambda: pl.semaphore_wait(barrier, XS + 3))
     pl.when(my_z >= 1)(lambda: tell(there, device(0, my_x)))
     pl.when(my_z >= 2)(lambda: tell(there, device(1, my_x)))
-    pl.when(~soon & (my_x != 0))(lambda: tell(x_there, device(my_z, 0)))
+    pl.when(~soon & (my_x != 0))(lambda: tell(x_there, hub))
 
     own_copy.wait()
     len_copy.wait()
@@ -111,10 +137,11 @@
             device_id_type=MESH,
         )
 
-    @pl.loop(0, ZS)
-    def _(k):
-        swap(turn(k), keys, k_buf, k_send, k_recv).start()
-        swap(turn(k), values, v_buf, v_send, v_recv).start()
+    def hand_over(k, z):
+        swap(z, keys, k_buf, k_send, k_recv).start()
+        swap(z, values, v_buf, v_send, v_recv).start()
+
+    in_order(hand_over)
 
     def arrived(z):
         def wait(n):
@@ -136,12 +163,13 @@
 
     @pl.when(~soon)
     def _():
-        @pl.when(my_x == 0)
+        @pl.when(me == hub)
         def _():
-            pl.semaphore_wait(x_there, XS - 1)
-            beside_x(lambda b: tell(x_all, b))
-
-        pl.when(my_x != 0)(lambda: pl.semaphore_wait(x_all, 1))
+            pl.semaphore_wait(x_there, (XS - 1) * CS)
+            spokes(lambda b: tell(x_all, b))
+            tell(x_all, beside)
+
+        pl.when(me != hub)(lambda: pl.semaphore_wait(x_all, 1))
         beside_x(ask)
 
     arrived(my_z)
@@ -159,7 +187,23 @@
     pl.when(my_z >= 2)(lambda: pl.semaphore_wait(column, 1))
     for step in FAR[:-1]:
         z = lax.rem(my_z + step, ZS)
-        pl.when(soon | (z != 0))(lambda z=z: bundle(device(z, my_x)))
+        pl.when(soon | (z >= SOON))(lambda z=z: bundle(device(z, my_x)))
+
+    late = pl.ds(SOON * XS, SOON * XS)
+
+    @pl.when(my_z == 0)
+    def _():
+        for z in range(SOON, ZS):
+            arrived(z)
+        for z in range(SOON - 1, 0, -1):
+            pltpu.make_async_remote_copy(
+                src_ref=q_buf.at[late],
+                dst_ref=q_buf.at[late],
+                send_sem=q_send,
+                recv_sem=late_recv,
+                device_id={"ctx": device(z, my_x)},
+                device_id_type=MESH,
+            ).start()
 
     k_copy.wait()
     v_copy.wait()
@@ -212,14 +256,17 @@
             device_id_type=MESH,
         ).start()
 
-    @pl.loop(0, ZS)
-    def _(k):
-        z = turn(k)
-        pl.when(z != my_z)(lambda: arrived(z))
+    def serve(k, z):
+        pl.when((z != my_z) & ((z < SOON) | ~soon))(lambda: arrived(z))
+        pl.when((k == SOON) & soon & (my_z != 0))(
+            lambda: pltpu.make_async_copy(q_buf.at[late], q_buf.at[late], late_recv).wait()
+        )
         swap(z, keys, k_buf, k_send, k_recv).wait_recv()
         swap(z, values, v_buf, v_send, v_recv).wait_recv()
         answer(z)
         in_plane(z, give)
+
+    in_order(serve)
 
     parts[chip] = part[chip]
 
@@ -235,7 +282,13 @@
         total += scale[:, s : s + 1] * parts[s, pl.ds(0, ROWS), :]
     out[...] = total.astype(out.dtype)
 
-    pltpu.make_async_copy(q_buf.at[rest], q_buf.at[rest], q_send).wait()
+    def left(n):
+        return lambda: pltpu.make_async_copy(q_buf.at[pl.ds(0, n)], q_buf.at[pl.ds(0, n)], q_send).wait()
+
+    pl.when(soon)(left(XS - 1 + (ZS - 1) * XS))
+    pl.when(~soon)(left(XS - 1 + XS + (SOON - 1) * XS))
+    for _ in range(1, SOON):
+        pl.when(my_z == 0)(left(SOON * XS))
     pltpu.make_async_copy(part.at[rest], part.at[rest], p_send).wait()
     pltpu.make_async_copy(k_buf.at[:, 0], k_buf.at[:, 0], k_send).wait()
     pltpu.make_async_copy(v_buf.at[:, 0], v_buf.at[:, 0], v_send).wait()
@@ -257,7 +310,7 @@
             pltpu.VMEM((CHIPS, ROWS + 1, SIZE), jnp.float32),
             pltpu.VMEM((CHIPS, ROWS + 1, SIZE), jnp.float32),
             dma, dma((ZS,)), dma, dma, dma, dma, dma, dma, dma((ZS,)), dma((ZS,)), dma((2,)),
-            *[pltpu.SemaphoreType.REGULAR] * 4,
+            *[pltpu.SemaphoreType.REGULAR] * 4, dma,
         ],
         compiler_params=pltpu.CompilerParams(collective_id=0, has_side_effects=True),
     )(

time: 21.2 us -> 21 us (level)
  the two profiles are of different devices: /device:TPU:8 before, /device:TPU:32 now
where the time goes in v6:
time: 21 us; the launch traced here: 20.9 us
  Pallas kernels  20.3 us (97%)
  local copies, waits for them, and re-layouts  0.58 us (3%)
    pallas_call x1, Pallas kernels, body(): pl.pallas_call(kernel, out_shape=pltpu.VMEM((ROWS, SIZE), jnp.bfloat16),...  20.3 us
    unnamed x1, local copies, waits for them, and re-layouts  0.58 us

profile of v6, /device:TPU:32, one launch (start us, length us, event | category | flops | bytes accessed | tf_op | source)
XLA Modules:
  0.0 20.9 jit_solution(2120515399768178985)
XLA Ops:
  0.0 20.3 %shard_map.46 = bf16[8,128]{1,0:T(8,128)(2,1)S(1)} custom-call(bf16[8,128]{1,0:T(8,128)(2,1)} %bitcast.7, bf16[32,2,256,128]{3,2,1,0:T(8,128)(2,1)} %bitcast.5, bf16[32,2,256,128]{3,2,1,0:T(8,128)(2,1)} %bitcast.6, s32[64]{0:T(128)} %lengths.1), custom_call_target="tpu_custom_call" | custom-call | tf_op jit(solution)/shard_map/pallas_call | solution.py:300
  20.3 0.6 %copy.6 = bf16[1,4,2,128]{3,2,1,0:T(2,128)(2,1)} copy(bf16[1,4,2,128]{3,2,1,0:T(2,128)(2,1)S(1)} %bitcast.4) | data formatting | bytes 4096
